TPU v7x, 32 devices: a whole 2x2x4 slice. The times are simulated.
32 devices in a mesh: gx: 2 (over y), gy: 4 (over z), gz: 4 (over x, core).
Axes of the slice: x: 2, y: 2, z: 4, core: 2. Of those that a mesh axis runs over, the one named last changes fastest.
Arguments:
- positions: float32 [2, 4, 4, 3, 48], P('gx', 'gy', 'gz'), may hold values from 0 to 1
- species: int32 [2, 4, 4, 48], P('gx', 'gy', 'gz'), may hold values from 0 to 3
- neighbours: int32 [2, 4, 4, 48, 128], P('gx', 'gy', 'gz'), may hold values from 0 to 1295
- neigh_counts: int32 [2, 4, 4, 48], P('gx', 'gy', 'gz'), may hold values from 64 to 128
- embedding: bfloat16 [4, 128], replicated, may hold values from -6 to 6
- rbf_decay: float32 [16], replicated, may hold values from 0.2 to 5
- radial_weight: bfloat16 [2, 16, 128], replicated, may hold values from -1.5 to 1.5
- node_weight: bfloat16 [2, 128, 128], replicated, may hold values from -0.5 to 0.5
- readout: bfloat16 [128], replicated, may hold values from -0.5 to 0.5
- species_bias: float32 [4], replicated, may hold values from -4 to 4
Outputs:
- atom_energy: float32 [2, 4, 4, 48], P('gx', 'gy', 'gz')
- total_energy: float32 [], replicated
Inputs may be any that keep to these rules, and one draw needn't show every extreme that they name: `neighbours`: the offset code of an entry is 9 (dx + 1) + 3 (dy + 1) + (dz + 1) for a cell offset of -1, 0 or 1 along each dimension.
All inputs are finite; a program needn't handle non-finite values.
Results may differ from a plain program's by a relative error of at most 0.0028.
Values may be sent and summed in bfloat16 or wider, within the bound.
A program may use at most 64 MiB of HBM per device.

v0:
```python
import jax
import jax.numpy as jnp
from jax import lax
from jax.sharding import PartitionSpec as P

LAYERS = 2


def extended_2(block, sides, width):
    for axis, dim in sides:
        count = lax.axis_size(axis)
        forward = [(i, i + 1) for i in range(count - 1)]
        forward.append((count - 1, 0))
        backward = [(target, source) for source, target in forward]
        low = lax.ppermute(
            lax.slice_in_dim(block, block.shape[dim] - width, None, axis=dim), axis, forward
        )
        high = lax.ppermute(lax.slice_in_dim(block, 0, width, axis=dim), axis, backward)
        block = jnp.concatenate([low, block, high], axis=dim)
    return block


def embed_atoms(species, embedding):
    kind_count = embedding.shape[0]
    one_hot = (species[..., None] == jnp.arange(kind_count, dtype=jnp.int32)).astype(jnp.bfloat16)
    embedded = jnp.dot(
        one_hot.reshape(-1, kind_count), embedding, preferred_element_type=jnp.float32
    )
    return embedded.astype(jnp.bfloat16).reshape(species.shape + (embedding.shape[1],))


def interaction(
    hidden_slab, place_slab, neighbour_row, count_row, rbf_decay, radial_weight, node_weight
):
    cell_count, slot_count, neighbour_count = neighbour_row.shape
    feature_width = hidden_slab.shape[-1]
    basis_count = rbf_decay.shape[0]
    slab_depth = cell_count + 2
    code_offset = neighbour_row // slot_count
    slot_index = neighbour_row % slot_count
    shift_x = code_offset // 9
    shift_y = code_offset // 3 % 3
    shift_z = code_offset % 3
    cell_column = lax.broadcasted_iota(jnp.int32, neighbour_row.shape, 0)
    cell_index = ((shift_x * 3 + shift_y) * slab_depth + cell_column + shift_z).reshape(-1)
    slot_flat = slot_index.reshape(-1)
    neighbour_feats = jnp.take(
        hidden_slab.reshape(-1, feature_width), cell_index * slot_count + slot_flat, axis=0
    )
    neighbour_feats = neighbour_feats.reshape(
        cell_count * slot_count, neighbour_count, feature_width
    )
    place_flat = place_slab.reshape(9 * slab_depth, 3, slot_count)
    far_place = place_flat[cell_index, :, slot_flat]
    centre = jnp.transpose(place_slab[1, 1, 1 : slab_depth - 1], (0, 2, 1))
    offsets_xyz = jnp.stack([shift_x - 1, shift_y - 1, shift_z - 1], axis=-1).astype(jnp.float32)
    displace = (
        far_place.reshape(cell_count, slot_count, neighbour_count, 3)
        + offsets_xyz
        - centre[:, :, None, :]
    )
    distance_sq = jnp.sum(displace * displace, axis=-1)
    radial_basis = jnp.exp(-distance_sq[..., None] * rbf_decay).astype(jnp.bfloat16)
    live_mask = lax.broadcasted_iota(jnp.int32, neighbour_row.shape, 2) < count_row[:, :, None]
    radial_basis = jnp.where(live_mask[..., None], radial_basis, jnp.bfloat16(0.0))
    radial_basis = radial_basis.reshape(cell_count * slot_count, neighbour_count, basis_count)
    collected = jnp.einsum(
        "anb,anf->abf", radial_basis, neighbour_feats, preferred_element_type=jnp.float32
    )
    message = jnp.sum(collected * radial_weight.astype(jnp.float32)[None], axis=1)
    inv_scale = lax.rsqrt(jnp.mean(message * message, axis=-1, keepdims=True) + 1e-05)
    normed = (message * inv_scale).astype(jnp.bfloat16)
    update = jax.nn.silu(jnp.dot(normed, node_weight, preferred_element_type=jnp.float32))
    own_rows = hidden_slab[1, 1, 1 : slab_depth - 1].reshape(-1, feature_width).astype(jnp.float32)
    return (own_rows + update).astype(jnp.bfloat16).reshape(cell_count, slot_count, feature_width)


def run_layer(
    hidden_pad, place_pad, neighbours, neigh_counts, rbf_decay, radial_weight, node_weight
):
    span_x = neighbours.shape[0]
    span_y = neighbours.shape[1]

    def one_row(row_index):
        row_x = row_index // span_y
        row_y = row_index % span_y
        return interaction(
            hidden_pad,
            place_pad,
            neighbours[row_x, row_y],
            neigh_counts[row_x, row_y],
            rbf_decay,
            radial_weight,
            node_weight,
        )

    row_results = lax.map(one_row, jnp.arange(span_x * span_y, dtype=jnp.int32))
    return row_results.reshape((span_x, span_y) + row_results.shape[1:])


def atom_energies(hidden, species, readout, species_bias):
    per_atom = jnp.sum(hidden.astype(jnp.float32) * readout.astype(jnp.float32), axis=-1)
    one_hot = (species[..., None] == jnp.arange(species_bias.shape[0], dtype=jnp.int32)).astype(
        jnp.float32
    )
    return per_atom + jnp.sum(one_hot * species_bias, axis=-1)


def body(
    positions,
    species,
    neighbours,
    neigh_counts,
    embedding,
    rbf_decay,
    radial_weight,
    node_weight,
    readout,
    species_bias,
):
    records = jnp.concatenate([positions, species.astype(jnp.float32)[:, :, :, None, :]], axis=3)
    extended = extended_2(records, (("gx", 0), ("gy", 1), ("gz", 2)), 1)
    place_pad = extended[:, :, :, 0:3]
    hidden_pad = embed_atoms(extended[:, :, :, 3].astype(jnp.int32), embedding)
    hidden = None
    for layer_index in range(LAYERS):
        if layer_index > 0:
            hidden_pad = extended_2(hidden, (("gx", 0), ("gy", 1), ("gz", 2)), 1)
        hidden = run_layer(
            hidden_pad,
            place_pad,
            neighbours,
            neigh_counts,
            rbf_decay,
            radial_weight[layer_index],
            node_weight[layer_index],
        )
    energy = atom_energies(hidden, species, readout, species_bias)
    total = lax.psum(jnp.sum(energy), ("gx", "gy", "gz"))
    return (energy, total)


def solution(mesh):
    return jax.shard_map(
        body,
        mesh=mesh,
        in_specs=(
            P("gx", "gy", "gz", None, None),
            P("gx", "gy", "gz", None),
            P("gx", "gy", "gz", None, None),
            P("gx", "gy", "gz", None),
            P(),
            P(),
            P(),
            P(),
            P(),
            P(),
        ),
        out_specs=(P("gx", "gy", "gz", None), P()),
        check_vma=False,
    )
```

profile of v0, /device:TPU:0, one launch (start us, length us, event | category | flops | bytes accessed | tf_op | source)
XLA Modules:
  0.0 190.2 jit_solution(17872462286565386704)
XLA Ops:
  0.6 0.7 convert_bitcast_fusion
  1.3 0.7 pad_maximum_fusion.6
  2.0 3.0 %collective-permute-start = (f32[1,1,1,4,48]{4,2,3,1,0:T(1,128)S(1)}, f32[1,1,1,4,48]{4,2,3,1,0:T(1,128)S(1)}, u32[]{:S(2)}, u32[]{:S(2)}) collective-permute-start(f32[1,1,1,4,48]{4,2,3,1,0:T(1,128)S(1)} %pad_maximum_fusion.6), channel_id=1, source_target_pairs={{0,16},{16,0},{1,17},{17,1},{2,18},{18,2},{3,19},{19,3},{4,20},{20... | collective-permute-start | bytes 2312 | tf_op jit(solution)/shard_map/ppermute | solution.py:15
  5.0 0.7 broadcast_divide_fusion
  5.8 0.8 compare_and_fusion
  6.6 0.2 broadcast_add_fusion.2
  6.8 0.3 broadcast_add_fusion.1
  7.1 0.3 fusion.34
  7.4 1.2 collective-permute-done.1
  8.6 0.7 pad_maximum_fusion.5
  9.3 1.6 collective-permute-start.2
  10.8 2.2 %collective-permute-start.3 = (f32[3,1,1,4,48]{4,2,3,1,0:T(1,128)S(1)}, f32[3,1,1,4,48]{4,2,3,1,0:T(1,128)S(1)}, u32[]{:S(2)}, u32[]{:S(2)}) collective-permute-start(f32[3,1,1,4,48]{4,2,3,1,0:T(1,128)S(1)} %pad_maximum_fusion.5), channel_id=1, source_target_pairs={{4,0},{8,4},{12,8},{0,12},{5,1},{9,5},{13,9},{1,13},{6,2},{10,6},{... | collective-permute-start | bytes 6920 | tf_op jit(solution)/shard_map/ppermute | solution.py:18
  13.1 0.7 bitcast_convert_fusion
  13.8 0.9 collective-permute-done.2
  14.7 0.7 pad_maximum_fusion.4
  15.5 1.7 collective-permute-start.5
  17.2 0.7 iota_compare_fusion.2
  17.9 0.7 copy.26
  18.7 0.7 pad_maximum_fusion.2
  19.4 0.3 copy.19
  19.7 66.4 %gather_fusion = f32[6144,3]{1,0:T(8,128)} fusion(f32[27,3,48]{1,2,0:T(8,128)S(1)} %bitcast.86, s32[6144]{0:T(1024)S(1)} %bitcast.89), kind=kCustom, calls=%fused_computation.2 | custom fusion | bytes 196608 | tf_op jit(solution)/shard_map/while/body/eval_jaxpr/gather | solution.py:54
  86.1 2.4 %copy.20 = f32[48,128,3]{1,0,2:T(8,128)S(1)} copy(f32[48,128,3]{2,1,0:T(8,128)} %bitcast.90) | data formatting | bytes 147456 | tf_op jit(solution)/shard_map/while/body/eval_jaxpr/gather | solution.py:54
  88.5 0.1 fusion.18
  88.7 0.4 convolution_convert_fusion
  89.1 18.1 %gather_fusion.1 = bf16[6144,128]{1,0:T(8,128)(2,1)S(1)} fusion(bf16[1296,128]{1,0:T(8,128)(2,1)S(1)} %convolution_convert_fusion, s32[6144]{0:T(1024)S(1)} %broadcast_clamp_fusion), kind=kCustom, calls=%fused_computation.clone | custom fusion | bytes 3170304 | tf_op jit(solution)/shard_map/while/body/eval_jaxpr/jit(_take)/gather | solution.py:47
  107.1 3.2 %broadcast_select_fusion.1 = bf16[6144,128]{1,0:T(8,128)(2,1)S(1)} fusion(bf16[6144,128]{1,0:T(8,128)(2,1)S(1)} %gather_fusion.1, pred[6144]{0:T(1024)(128)(4,1)S(1)} %get-tuple-element.48), kind=kLoop, calls=%fused_computation.5 | loop fusion | flops 786432 | bytes 3151872 | tf_op jit(solution)/shard_map/while/body/eval_jaxpr/jit(_take)/select_n | solution.py:47
  110.4 0.6 fusion
  111.0 0.1 multiply_reduce_fusion.2
  111.2 0.2 fusion.37
  111.4 0.9 collective-permute-start.6
  112.3 1.2 collective-permute-start.7
  113.5 1.7 collective-permute-done.6
  115.2 0.8 collective-permute-done.7
  116.0 1.3 collective-permute-start.8
  117.4 2.5 %collective-permute-start.9 = (bf16[3,1,1,48,128]{4,3,2,1,0:T(8,128)(2,1)S(1)}, bf16[3,1,1,48,128]{4,3,2,1,0:T(8,128)(2,1)S(1)}, u32[]{:S(2)}, u32[]{:S(2)}) collective-permute-start(bf16[3,1,1,48,128]{4,3,2,1,0:T(8,128)(2,1)S(1)} %pad_maximum_fusion.3), channel_id=1, source_target_pairs={{4,0},{8,4},{12,8},{0,12},{5,1},{9,5},{13,9},{1,13},{6,2},{10,6},{... | collective-permute-start | bytes 110600 | tf_op jit(solution)/shard_map/ppermute | solution.py:18
  119.9 1.9 collective-permute-done.8
  121.8 0.2 collective-permute-done.9
  122.1 1.7 collective-permute-start.11
  123.9 0.1 select_reduce_fusion
  124.0 2.3 %collective-permute-done.10 = bf16[3,3,1,48,128]{4,3,2,1,0:T(8,128)(2,1)S(1)} collective-permute-done((bf16[3,3,1,48,128]{4,3,2,1,0:T(8,128)(2,1)S(1)}, bf16[3,3,1,48,128]{4,3,2,1,0:T(8,128)(2,1)S(1)}, u32[]{:S(2)}, u32[]{:S(2)}) %collective-permute-start.10) | collective-permute-done | bytes 110624 | tf_op jit(solution)/shard_map/ppermute | solution.py:15
  126.3 0.3 collective-permute-done.11
  126.6 18.1 %gather_fusion.2 = bf16[6144,128]{1,0:T(8,128)(2,1)S(1)} fusion(bf16[1296,128]{1,0:T(8,128)(2,1)S(1)} %bitcast.88, s32[6144]{0:T(1024)S(1)} %broadcast_clamp_fusion), kind=kCustom, calls=%fused_computation.1.clone | custom fusion | bytes 3170304 | tf_op jit(solution)/shard_map/while/body/eval_jaxpr/jit(_take)/gather | solution.py:47
  144.7 3.2 %broadcast_select_fusion = bf16[6144,128]{1,0:T(8,128)(2,1)S(1)} fusion(bf16[6144,128]{1,0:T(8,128)(2,1)S(1)} %gather_fusion.2, pred[6144]{0:T(1024)(128)(4,1)S(1)} %get-tuple-element.48), kind=kLoop, calls=%fused_computation.4 | loop fusion | flops 786432 | bytes 3151872 | tf_op jit(solution)/shard_map/while/body/eval_jaxpr/jit(_take)/select_n | solution.py:47
  147.9 0.6 fusion.1
  148.6 0.1 multiply_reduce_fusion.1
  148.7 0.3 multiply_reduce_fusion
  149.0 1.1 add_reduce_fusion
  150.1 40.1 %psum.7 = f32[]{:T(128)} all-reduce(f32[]{:T(128)} %get-tuple-element.66), channel_id=1, replica_groups=mesh['gx'=2,'gy'=4,'gz'=4] {'gx','gy','gz'}, use_global_device_ids=true, to_apply=%region_8.10 | all-reduce | flops 1 | bytes 8 | tf_op jit(solution)/shard_map/psum | solution.py:139
  (30 shorter events, 0.5 us)
Async XLA Ops:
  0.6 88.1 %copy-start = (bf16[4,128]{1,0:T(4,128)(2,1)S(1)}, bf16[4,128]{1,0:T(4,128)(2,1)}, u32[]{:S(2)}) copy-start(bf16[4,128]{1,0:T(4,128)(2,1)} %param.16) | copy-start | bytes 3076
  2.0 5.4 %collective-permute-start = (f32[1,1,1,4,48]{4,2,3,1,0:T(1,128)S(1)}, f32[1,1,1,4,48]{4,2,3,1,0:T(1,128)S(1)}, u32[]{:S(2)}, u32[]{:S(2)}) collective-permute-start(f32[1,1,1,4,48]{4,2,3,1,0:T(1,128)S(1)} %pad_maximum_fusion.6), channel_id=1, source_target_pairs={{0,16},{16,0},{1,17},{17,1},{2,18},{18,2},{3,19},{19,3},{4,20},{20... | collective-permute-start | bytes 2312 | tf_op jit(solution)/shard_map/ppermute | solution.py:15
  5.0 3.6 %collective-permute-start.1 = (f32[1,1,1,4,48]{4,2,3,1,0:T(1,128)S(1)}, f32[1,1,1,4,48]{4,2,3,1,0:T(1,128)S(1)}, u32[]{:S(2)}, u32[]{:S(2)}) collective-permute-start(f32[1,1,1,4,48]{4,2,3,1,0:T(1,128)S(1)} %pad_maximum_fusion.6), channel_id=1, source_target_pairs={{16,0},{0,16},{17,1},{1,17},{18,2},{2,18},{19,3},{3,19},{20,4},{4,... | collective-permute-start | bytes 2312 | tf_op jit(solution)/shard_map/ppermute | solution.py:18
  9.3 5.4 %collective-permute-start.2 = (f32[3,1,1,4,48]{4,2,3,1,0:T(1,128)S(1)}, f32[3,1,1,4,48]{4,2,3,1,0:T(1,128)S(1)}, u32[]{:S(2)}, u32[]{:S(2)}) collective-permute-start(f32[3,1,1,4,48]{4,2,3,1,0:T(1,128)S(1)} %pad_maximum_fusion.5), channel_id=1, source_target_pairs={{0,4},{4,8},{8,12},{12,0},{1,5},{5,9},{9,13},{13,1},{2,6},{6,10},{... | collective-permute-start | bytes 6920 | tf_op jit(solution)/shard_map/ppermute | solution.py:15
  10.8 3.9 %collective-permute-start.3 = (f32[3,1,1,4,48]{4,2,3,1,0:T(1,128)S(1)}, f32[3,1,1,4,48]{4,2,3,1,0:T(1,128)S(1)}, u32[]{:S(2)}, u32[]{:S(2)}) collective-permute-start(f32[3,1,1,4,48]{4,2,3,1,0:T(1,128)S(1)} %pad_maximum_fusion.5), channel_id=1, source_target_pairs={{4,0},{8,4},{12,8},{0,12},{5,1},{9,5},{13,9},{1,13},{6,2},{10,6},{... | collective-permute-start | bytes 6920 | tf_op jit(solution)/shard_map/ppermute | solution.py:18
  15.4 3.2 %collective-permute-start.4 = (f32[3,3,1,4,48]{4,2,3,1,0:T(1,128)S(1)}, f32[3,3,1,4,48]{4,2,3,1,0:T(1,128)S(1)}, u32[]{:S(2)}, u32[]{:S(2)}) collective-permute-start(f32[3,3,1,4,48]{4,2,3,1,0:T(1,128)S(1)} %pad_maximum_fusion.4), channel_id=1, source_target_pairs={{0,1},{1,2},{2,3},{3,0},{4,5},{5,6},{6,7},{7,4},{8,9},{9,10},{10,1... | collective-permute-start | bytes 20744 | tf_op jit(solution)/shard_map/ppermute | solution.py:15
  15.5 3.2 %collective-permute-start.5 = (f32[3,3,1,4,48]{4,2,3,1,0:T(1,128)S(1)}, f32[3,3,1,4,48]{4,2,3,1,0:T(1,128)S(1)}, u32[]{:S(2)}, u32[]{:S(2)}) collective-permute-start(f32[3,3,1,4,48]{4,2,3,1,0:T(1,128)S(1)} %pad_maximum_fusion.4), channel_id=1, source_target_pairs={{1,0},{2,1},{3,2},{0,3},{5,4},{6,5},{7,6},{4,7},{9,8},{10,9},{11,1... | collective-permute-start | bytes 20744 | tf_op jit(solution)/shard_map/ppermute | solution.py:18
  107.1 3.3 %copy-start.1 = (f32[16]{0:T(128)S(1)}, f32[16]{0:T(128)}, u32[]{:S(2)}) copy-start(f32[16]{0:T(128)} %param.17) | copy-start | bytes 196
  110.4 0.8 copy-start.2
  110.4 9.5 %copy-start.3 = (bf16[128]{0:T(256)(128)(2,1)S(1)}, bf16[128]{0:T(256)(128)(2,1)}, u32[]{:S(2)}) copy-start(bf16[128]{0:T(256)(128)(2,1)} %param.20) | copy-start | bytes 772
  110.4 13.5 %copy-start.4 = (s32[1,1,1,48]{3,2,1,0:T(1,128)S(1)}, s32[1,1,1,48]{3,2,1,0:T(1,128)}, u32[]{:S(2)}) copy-start(s32[1,1,1,48]{3,2,1,0:T(1,128)} %param.13) | copy-start | bytes 580
  110.4 13.5 %copy-start.5 = (f32[4]{0:T(128)S(1)}, f32[4]{0:T(128)}, u32[]{:S(2)}) copy-start(f32[4]{0:T(128)} %param.21) | copy-start | bytes 52
  111.4 3.8 %collective-permute-start.6 = (bf16[1,1,1,48,128]{4,3,2,1,0:T(8,128)(2,1)S(1)}, bf16[1,1,1,48,128]{4,3,2,1,0:T(8,128)(2,1)S(1)}, u32[]{:S(2)}, u32[]{:S(2)}) collective-permute-start(bf16[1,1,1,48,128]{4,3,2,1,0:T(8,128)(2,1)S(1)} %bitcast.95), channel_id=1, source_target_pairs={{0,16},{16,0},{1,17},{17,1},{2,18},{18,2},{3,19},{19,3},{4,20},{20... | collective-permute-start | bytes 36872 | tf_op jit(solution)/shard_map/ppermute | solution.py:15
  112.3 3.7 %collective-permute-start.7 = (bf16[1,1,1,48,128]{4,3,2,1,0:T(8,128)(2,1)S(1)}, bf16[1,1,1,48,128]{4,3,2,1,0:T(8,128)(2,1)S(1)}, u32[]{:S(2)}, u32[]{:S(2)}) collective-permute-start(bf16[1,1,1,48,128]{4,3,2,1,0:T(8,128)(2,1)S(1)} %bitcast.96), channel_id=1, source_target_pairs={{16,0},{0,16},{17,1},{1,17},{18,2},{2,18},{19,3},{3,19},{20,4},{4,... | collective-permute-start | bytes 36872 | tf_op jit(solution)/shard_map/ppermute | solution.py:18
  116.0 5.8 %collective-permute-start.8 = (bf16[3,1,1,48,128]{4,3,2,1,0:T(8,128)(2,1)S(1)}, bf16[3,1,1,48,128]{4,3,2,1,0:T(8,128)(2,1)S(1)}, u32[]{:S(2)}, u32[]{:S(2)}) collective-permute-start(bf16[3,1,1,48,128]{4,3,2,1,0:T(8,128)(2,1)S(1)} %pad_maximum_fusion.3), channel_id=1, source_target_pairs={{0,4},{4,8},{8,12},{12,0},{1,5},{5,9},{9,13},{13,1},{2,6},{6,10},{... | collective-permute-start | bytes 110600 | tf_op jit(solution)/shard_map/ppermute | solution.py:15
  117.4 4.7 %collective-permute-start.9 = (bf16[3,1,1,48,128]{4,3,2,1,0:T(8,128)(2,1)S(1)}, bf16[3,1,1,48,128]{4,3,2,1,0:T(8,128)(2,1)S(1)}, u32[]{:S(2)}, u32[]{:S(2)}) collective-permute-start(bf16[3,1,1,48,128]{4,3,2,1,0:T(8,128)(2,1)S(1)} %pad_maximum_fusion.3), channel_id=1, source_target_pairs={{4,0},{8,4},{12,8},{0,12},{5,1},{9,5},{13,9},{1,13},{6,2},{10,6},{... | collective-permute-start | bytes 110600 | tf_op jit(solution)/shard_map/ppermute | solution.py:18
  122.1 4.2 %collective-permute-start.10 = (bf16[3,3,1,48,128]{4,3,2,1,0:T(8,128)(2,1)S(1)}, bf16[3,3,1,48,128]{4,3,2,1,0:T(8,128)(2,1)S(1)}, u32[]{:S(2)}, u32[]{:S(2)}) collective-permute-start(bf16[3,3,1,48,128]{4,3,2,1,0:T(8,128)(2,1)S(1)} %pad_maximum_fusion.1), channel_id=1, source_target_pairs={{0,1},{1,2},{2,3},{3,0},{4,5},{5,6},{6,7},{7,4},{8,9},{9,10},{10,1... | collective-permute-start | bytes 331784 | tf_op jit(solution)/shard_map/ppermute | solution.py:15
  122.1 4.5 %collective-permute-start.11 = (bf16[3,3,1,48,128]{4,3,2,1,0:T(8,128)(2,1)S(1)}, bf16[3,3,1,48,128]{4,3,2,1,0:T(8,128)(2,1)S(1)}, u32[]{:S(2)}, u32[]{:S(2)}) collective-permute-start(bf16[3,3,1,48,128]{4,3,2,1,0:T(8,128)(2,1)S(1)} %pad_maximum_fusion.1), channel_id=1, source_target_pairs={{1,0},{2,1},{3,2},{0,3},{5,4},{6,5},{7,6},{4,7},{9,8},{10,9},{11,1... | collective-permute-start | bytes 331784 | tf_op jit(solution)/shard_map/ppermute | solution.py:18
where the time goes:
time: 191 us; the launch traced here: 190 us
  local copies, waits for them, and re-layouts  106 us (55%)
  blocking collectives  40.1 us (21%)
  starting transfers between devices  16.4 us (9%)
  other arithmetic  15.3 us (8%)
  waiting for transfers between devices  9.4 us (5%)
  matrix products  2.07 us (1%)
    gather x2, local copies, waits for them, and re-layouts, interaction(): far_place = place_flat[cell_index, :, slot_flat]  68.7 us
    psum x1, blocking collectives, body(): total = lax.psum(jnp.sum(energy), ('gx', 'gy', 'gz'))  40.1 us
    gather x2, local copies, waits for them, and re-layouts, interaction(): jnp.take(hidden_slab.reshape(-1, feature_width), cell_index * slot_count...  36.2 us
    ppermute x6, starting transfers between devices, extended_2(): lax.ppermute(lax.slice_in_dim(block, 0, width, axis=dim), axis, backward)  9.45 us
    ppermute x6, starting transfers between devices, extended_2(): lax.ppermute(lax.slice_in_dim(block, block.shape[dim] - width, None, axis...  6.95 us
    ppermute x6, waiting for transfers between devices, extended_2(): lax.ppermute(lax.slice_in_dim(block, block.shape[dim] - width, None, axis...  6.8 us
    select_n x2, other arithmetic, interaction(): jnp.take(hidden_slab.reshape(-1, feature_width), cell_index * slot_count...  6.42 us
  transfers between devices with their start and end apart: 12, of which 8 were waited for; matrix products, arithmetic and copies ran while one was open for 2% of the time, Pallas kernels for 0%

commit v1 on v0

v1 whole, which is shorter than its diff:
```python
import functools
import itertools
import math

import jax
import jax.numpy as jnp
from jax import lax
from jax.experimental import pallas as pl
from jax.experimental.pallas import tpu as pltpu
from jax.sharding import PartitionSpec as P

AXES = ("gx", "gy", "gz")
MESH = pl.DeviceIdType.MESH
LANES = 128
LOG2E = math.log2(math.e)


def distinct(count):
    return (0,) if count == 1 else (0, -1) if count == 2 else (0, -1, 1)


def canonical(offset, count):
    return 0 if count == 1 else -abs(offset) if count == 2 else offset


def code_of(offset):
    return 9 * (offset[0] + 1) + 3 * (offset[1] + 1) + offset[2] + 1


def kernel(
    sizes,
    stages,
    pos_ref,
    spec_ref,
    nbr_ref,
    cnt_ref,
    emb_ref,
    decay_ref,
    radial_ref,
    node_ref,
    readout_ref,
    bias_ref,
    energy_ref,
    total_ref,
    record,
    places,
    hist,
    codes,
    basis,
    feats0,
    feats1,
    *rest,
):
    stage_bufs = rest[: len(stages)]
    pos_send, pos_recv, hid_send, hid_recv = rest[len(stages) : len(stages) + 4]
    stage_sems = rest[len(stages) + 4 :]
    me = tuple(lax.axis_index(name) for name in AXES)
    slots = pos_ref.shape[-1]
    neighbour_count = nbr_ref.shape[-1]
    features = emb_ref.shape[1]
    kinds = emb_ref.shape[0]
    basis_count = radial_ref.shape[1]
    layers = radial_ref.shape[0]
    tiles = basis.shape[1] // LANES
    hi_rows = hist.shape[0] // slots

    def device(shift):
        return tuple(
            lax.rem(coord + (delta % count), count) if delta % count else coord
            for coord, delta, count in zip(me, shift, sizes)
        )

    neighbours = [
        off for off in itertools.product(*(distinct(n) for n in sizes)) if off != (0, 0, 0)
    ]
    stage_shifts = [
        [
            shift
            for shift in itertools.product(
                *(range(n) if name in axes else (0,) for name, n in zip(AXES, sizes))
            )
            if any(shift)
        ]
        for axes in stages
    ]
    partners = {tuple((-d) % n for d, n in zip(off, sizes)) for off in neighbours}
    for shifts in stage_shifts:
        partners.update(shifts)
    barrier = pltpu.get_barrier_semaphore()
    for shift in sorted(partners):
        pl.semaphore_signal(barrier, inc=1, device_id=device(shift), device_id_type=MESH)

    record[...] = jnp.zeros(record.shape, jnp.float32)
    record[0:3, 0:slots] = pos_ref[0, 0, 0]
    record[3:4, 0:slots] = spec_ref[0, 0].astype(jnp.float32)
    record[4:5, 0:slots] = cnt_ref[0, 0].astype(jnp.float32)
    columns = jnp.transpose(record[...])[0:slots]
    own_pos = [
        jnp.broadcast_to(columns[:, c : c + 1], (slots, LANES)) for c in range(3)
    ]
    species_col = columns[:, 3:4]
    count_col = columns[:, 4:5]

    pl.semaphore_wait(barrier, len(partners))

    def place_copy(off):
        code = code_of(off)
        return pltpu.make_async_remote_copy(
            src_ref=record,
            dst_ref=places.at[code],
            send_sem=pos_send.at[code],
            recv_sem=pos_recv.at[code],
            device_id=device(tuple(-d for d in off)),
            device_id_type=MESH,
        )

    place_copies = [place_copy(off) for off in neighbours]
    for copy in place_copies:
        copy.start()

    raw = nbr_ref[0, 0, 0]
    live = lax.broadcasted_iota(jnp.int32, raw.shape, 1).astype(jnp.float32) < count_col
    codes[...] = jnp.where(live, raw, hi_rows * LANES - 1)
    hi_iota = lax.broadcasted_iota(jnp.int32, (hi_rows, neighbour_count), 0)
    lo_iota = lax.broadcasted_iota(jnp.int32, (LANES, neighbour_count), 0)
    for atom in range(slots):
        row = codes[atom : atom + 1, :]
        high = jnp.where((row >> 7) == hi_iota, 1.0, 0.0).astype(jnp.bfloat16)
        low = jnp.where((row & (LANES - 1)) == lo_iota, 1.0, 0.0).astype(jnp.bfloat16)
        hist[atom * hi_rows : (atom + 1) * hi_rows, :] = lax.dot_general(
            high, low, (((1,), (1,)), ((), ())), preferred_element_type=jnp.float32
        )

    own_hidden = jnp.zeros((slots, features), jnp.float32)
    for kind in range(kinds):
        own_hidden = jnp.where(
            species_col == float(kind), emb_ref[kind : kind + 1, :].astype(jnp.float32), own_hidden
        )
    table_rows = feats1.shape[0]
    feats1[27 * slots : table_rows, :] = jnp.zeros(
        (table_rows - 27 * slots, features), jnp.bfloat16
    )
    emb = emb_ref[...].astype(jnp.float32)
    if kinds < 8:
        emb = jnp.concatenate([emb, jnp.zeros((8 - kinds, features), jnp.float32)], axis=0)
    emb = emb.astype(jnp.bfloat16)
    scales = [decay_ref[b] * (-LOG2E) for b in range(basis_count)]

    lane = lax.broadcasted_iota(jnp.int32, (8, LANES), 1)
    sub = lax.broadcasted_iota(jnp.int32, (8, LANES), 0)
    for copy in place_copies:
        copy.wait_recv()

    flat = [jnp.zeros((8, LANES), jnp.float32) for _ in range(tiles)]
    for off in itertools.product((-1, 0, 1), repeat=3):
        source = tuple(canonical(d, n) for d, n in zip(off, sizes))
        cell = record[...] if source == (0, 0, 0) else places[code_of(source)]
        for component, delta in enumerate(off):
            if delta:
                cell = jnp.where(sub == component, cell + float(delta), cell)
        tile, start = divmod(code_of(off) * slots, LANES)
        if start:
            cell = pltpu.roll(cell, start, 1)
        stop = start + slots
        flat[tile] = jnp.where((lane >= start) & (lane < stop), cell, flat[tile])
        if stop > LANES:
            flat[tile + 1] = jnp.where(lane < stop - LANES, cell, flat[tile + 1])

    for tile in range(tiles):
        span = slice(tile * LANES, (tile + 1) * LANES)
        r2 = jnp.zeros((slots, LANES), jnp.float32)
        for c in range(3):
            delta = flat[tile][c : c + 1, :] - own_pos[c]
            r2 = r2 + delta * delta
        times = hist[pl.ds(tile, slots, stride=hi_rows), :]
        for b in range(basis_count):
            basis[b * slots : (b + 1) * slots, span] = (
                jnp.exp2(r2 * scales[b]) * times
            ).astype(jnp.bfloat16)
        one_hot = jnp.where(
            flat[tile][3:4, :].astype(jnp.int32) == sub, 1.0, 0.0
        )
        feats0[span, :] = jnp.dot(
            jnp.transpose(one_hot).astype(jnp.bfloat16), emb, preferred_element_type=jnp.float32
        ).astype(jnp.bfloat16)

    def interaction(layer, feats, hidden):
        collected = jnp.dot(basis[...], feats[...], preferred_element_type=jnp.float32)
        weight = radial_ref[layer].astype(jnp.float32)
        message = jnp.zeros((slots, features), jnp.float32)
        for b in range(basis_count):
            message = message + collected[b * slots : (b + 1) * slots] * weight[b : b + 1]
        inv_scale = lax.rsqrt(jnp.mean(message * message, axis=-1, keepdims=True) + 1e-05)
        normed = (message * inv_scale).astype(jnp.bfloat16)
        value = jnp.dot(normed, node_ref[layer], preferred_element_type=jnp.float32)
        update = value / (1.0 + jnp.exp(-value))
        return (hidden + update).astype(jnp.bfloat16)

    hidden1 = interaction(0, feats0, own_hidden)
    own_rows = pl.ds(code_of((0, 0, 0)) * slots, slots)
    feats1[own_rows, :] = hidden1

    def hidden_copy(off):
        code = code_of(off)
        return pltpu.make_async_remote_copy(
            src_ref=feats1.at[own_rows],
            dst_ref=feats1.at[pl.ds(code * slots, slots)],
            send_sem=hid_send.at[code],
            recv_sem=hid_recv.at[code],
            device_id=device(tuple(-d for d in off)),
            device_id_type=MESH,
        )

    hidden_copies = [hidden_copy(off) for off in neighbours]
    for copy in hidden_copies:
        copy.start()

    species_row = record[3:4, :]
    offsets = jnp.zeros((1, LANES), jnp.float32)
    for kind in range(kinds):
        offsets = jnp.where(species_row == float(kind), bias_ref[kind], offsets)
    offsets = jnp.where(lane[0:1] < slots, offsets, 0.0)

    for copy in hidden_copies:
        copy.wait_recv()
    for off in itertools.product((-1, 0, 1), repeat=3):
        source = tuple(canonical(d, n) for d, n in zip(off, sizes))
        if source != off:
            feats1[pl.ds(code_of(off) * slots, slots), :] = feats1[
                pl.ds(code_of(source) * slots, slots), :
            ]
    hidden2 = interaction(1, feats1, hidden1.astype(jnp.float32))
    padded = jnp.concatenate(
        [hidden2, jnp.zeros((LANES - slots, features), jnp.bfloat16)], axis=0
    )
    readout = jnp.broadcast_to(readout_ref[...], (16, features))
    per_atom = lax.dot_general(
        readout, padded, (((1,), (1,)), ((), ())), preferred_element_type=jnp.float32
    )
    running = per_atom[0:1, :] + offsets
    energy_ref[0, 0] = running[:, 0:slots]

    for axes, shifts, buf, send, recv in zip(
        stages, stage_shifts, stage_bufs, stage_sems[0::2], stage_sems[1::2]
    ):
        def rank_of(coords):
            rank = 0
            for name, coord, count in zip(AXES, coords, sizes):
                if name in axes:
                    rank = rank * count + coord
            return rank

        mine = rank_of(me)
        buf[mine] = running
        copies = []
        for index, shift in enumerate(shifts):
            copies.append(
                pltpu.make_async_remote_copy(
                    src_ref=buf.at[mine],
                    dst_ref=buf.at[mine],
                    send_sem=send.at[index],
                    recv_sem=recv.at[index],
                    device_id=device(shift),
                    device_id_type=MESH,
                )
            )
        for copy in copies:
            copy.start()
        for copy in copies:
            copy.wait_recv()
        running = jnp.sum(buf[...], axis=0)
        for copy in copies:
            copy.wait_send()
    total_ref[...] = jnp.sum(running, axis=1, keepdims=True)
    for copy in place_copies + hidden_copies:
        copy.wait_send()


def body(sizes, *args):
    positions, species, neighbours, _, embedding, decay, radial, _, readout, _ = args
    slots = positions.shape[-1]
    features = embedding.shape[1]
    basis_count = decay.shape[0]
    tiles = pl.cdiv(27 * slots, LANES)
    hi_rows = 16 * pl.cdiv(tiles + 1, 16)
    devices = math.prod(sizes)
    stages = (AXES,) if devices <= 64 else tuple((name,) for name in AXES)
    stage_ranks = [
        math.prod(n for name, n in zip(AXES, sizes) if name in axes) for axes in stages
    ]
    vmem = pl.BlockSpec(memory_space=pltpu.VMEM)
    smem = pl.BlockSpec(memory_space=pltpu.SMEM)
    dma = pltpu.SemaphoreType.DMA
    scratch = [
        pltpu.VMEM((8, LANES), jnp.float32),
        pltpu.VMEM((27, 8, LANES), jnp.float32),
        pltpu.VMEM((slots * hi_rows, LANES), jnp.float32),
        pltpu.VMEM((slots, neighbours.shape[-1]), jnp.int32),
        pltpu.VMEM((basis_count * slots, tiles * LANES), jnp.bfloat16),
        pltpu.VMEM((tiles * LANES, features), jnp.bfloat16),
        pltpu.VMEM((tiles * LANES, features), jnp.bfloat16),
    ]
    scratch += [pltpu.VMEM((count, 1, LANES), jnp.float32) for count in stage_ranks]
    scratch += [dma((27,))] * 4
    for count in stage_ranks:
        scratch += [dma((max(count - 1, 1),))] * 2
    energy, total = pl.pallas_call(
        functools.partial(kernel, sizes, stages),
        out_shape=(
            jax.ShapeDtypeStruct(species.shape, jnp.float32),
            jax.ShapeDtypeStruct((1, 1), jnp.float32),
        ),
        in_specs=[vmem, vmem, vmem, vmem, vmem, smem, vmem, vmem, vmem, smem],
        out_specs=(vmem, vmem),
        scratch_shapes=scratch,
        compiler_params=pltpu.CompilerParams(collective_id=0, has_side_effects=True),
    )(*args[:8], readout.reshape(1, features), args[9])
    return energy, total.reshape(())


def solution(mesh):
    sizes = tuple(mesh.shape[name] for name in AXES)
    return jax.shard_map(
        functools.partial(body, sizes),
        mesh=mesh,
        in_specs=(
            P("gx", "gy", "gz", None, None),
            P("gx", "gy", "gz", None),
            P("gx", "gy", "gz", None, None),
            P("gx", "gy", "gz", None),
            P(),
            P(),
            P(),
            P(),
            P(),
            P(),
        ),
        out_specs=(P("gx", "gy", "gz", None), P()),
        check_vma=False,
    )
```

time: 191 us -> 32.1 us (0.17)
  local copies, waits for them, and re-layouts: 106 us -> 2.39 us
  blocking collectives: 40.1 us -> 0 us
  Pallas kernels: 0 us -> 27.1 us
  starting transfers between devices: 16.4 us -> 0 us
  other arithmetic: 15.3 us -> 0 us
  waiting for transfers between devices: 9.4 us -> 0 us
  matrix products: 2.07 us -> 0 us
    gather x4 -> x0, local copies, waits for them, and re-layouts: 105 us -> none  [the longest x2 68.7 us: interaction(): far_place = place_flat[cell_index, :, slot_flat]]
    psum x1 -> x0, blocking collectives: 40.1 us -> none  [body(): total = lax.psum(jnp.sum(energy), ('gx', 'gy', 'gz'))]
    pallas_call x0 -> x1, Pallas kernels: none -> 27.1 us  [body(): pl.pallas_call(functools.partial(kernel, sizes, stages), out_shape=(jax.S...]
    ppermute x12 -> x0, starting transfers between devices: 16.4 us -> none  [the longest x6 9.45 us: extended_2(): lax.ppermute(lax.slice_in_dim(block, 0, width, axis=dim), axis, backward)]
    ppermute x12 -> x0, waiting for transfers between devices: 9.4 us -> none  [the longest x6 6.8 us: extended_2(): lax.ppermute(lax.slice_in_dim(block, block.shape[dim] - width, None, axis...]
    select_n x2 -> x0, other arithmetic: 6.42 us -> none  [interaction(): jnp.take(hidden_slab.reshape(-1, feature_width), cell_index * slot_count...]
    concatenate x8 -> x0, other arithmetic: 3.15 us -> none  [the longest x6 2.2 us: extended_2(): block = jnp.concatenate([low, block, high], axis=dim)]
    dot_general x5 -> x0, matrix products: 2.07 us -> none  [the longest x2 1.19 us: interaction(): jnp.einsum('anb,anf->abf', radial_basis, neighbour_feats, preferred_eleme...]
  transfers between devices with their start and end apart: 12 -> 0, of which waited for: 8 -> 0; matrix products, arithmetic and copies ran while one was open for 2% -> 0% of each run, Pallas kernels for 0% -> 0%
where the time goes in v1:
time: 32.1 us; the launch traced here: 31.9 us
  Pallas kernels  27.1 us (84%)
  between operations  2.4 us (7%)
  local copies, waits for them, and re-layouts  2.39 us (7%)
    pallas_call x1, Pallas kernels, body(): pl.pallas_call(functools.partial(kernel, sizes, stages), out_shape=(jax.S...  27.1 us
    unnamed x6, local copies, waits for them, and re-layouts  2.39 us

profile of v1, /device:TPU:0, one launch (start us, length us, event | category | flops | bytes accessed | tf_op | source)
XLA Modules:
  0.0 31.9 jit_solution(6362008158336687326)
XLA Ops:
  0.6 0.0 copy-start
  0.6 0.7 %copy-done = f32[1,1,1,3,48]{4,2,3,1,0:T(1,128)S(1)} copy-done((f32[1,1,1,3,48]{4,2,3,1,0:T(1,128)S(1)}, f32[1,1,1,3,48]{4,2,3,1,0:T(1,128)}, u32[]{:S(2)}) %copy-start) | copy-done | bytes 600
  1.3 0.6 %copy.12.pos_ref = f32[1,1,1,3,48]{4,3,2,1,0:T(4,128)} copy(f32[1,1,1,3,48]{4,2,3,1,0:T(1,128)S(1)} %copy-done) | data formatting | bytes 1152 | tf_op args[0]
  1.9 27.1 %shard_map.113 = (f32[1,1,1,48]{3,2,1,0:T(1,128)}, f32[1,1]{1,0:T(1,128)}) custom-call(f32[1,1,1,3,48]{4,3,2,1,0:T(4,128)} %copy.12.pos_ref, s32[1,1,1,48]{3,2,1,0:T(1,128)} %spec_ref.1, s32[1,1,1,48,128]{4,3,2,1,0:T(8,128)} %nbr_ref.1, s32[1,1,1,48]{3,2,1,0:T(1,128)} %cnt_ref.1, bf16[4,128]{1,0:T(4,128)(2,1)} %emb_ref.1, f32[16]{0:T(128)} %decay_ref.1, ...), custom_call_target="tpu_custom_call" | custom-call | tf_op jit(solution)/shard_map/pallas_call | solution.py:307
  29.0 0.0 copy-start.1
  29.0 0.6 %copy-done.1 = f32[1,1,1,48]{3,2,1,0:T(1,128)S(1)} copy-done((f32[1,1,1,48]{3,2,1,0:T(1,128)S(1)}, f32[1,1,1,48]{3,2,1,0:T(1,128)}, u32[]{:S(2)}) %copy-start.1) | copy-done | bytes 216
  29.6 0.5 %copy.15 = f32[1,1,1,48]{3,2,1,0:T(1,128)} copy(f32[1,1,1,48]{3,2,1,0:T(1,128)S(1)} %copy-done.1) | data formatting | bytes 384
Async XLA Ops:
  0.6 0.7 %copy-start = (f32[1,1,1,3,48]{4,2,3,1,0:T(1,128)S(1)}, f32[1,1,1,3,48]{4,2,3,1,0:T(1,128)}, u32[]{:S(2)}) copy-start(f32[1,1,1,3,48]{4,2,3,1,0:T(1,128)} %param.10) | copy-start | bytes 1732
  29.0 0.6 %copy-start.1 = (f32[1,1,1,48]{3,2,1,0:T(1,128)S(1)}, f32[1,1,1,48]{3,2,1,0:T(1,128)}, u32[]{:S(2)}) copy-start(f32[1,1,1,48]{3,2,1,0:T(1,128)} %get-tuple-element.8) | copy-start | bytes 580

commit v2 on v1

--- a/solution.py
+++ b/solution.py
@@ -27,21 +27,27 @@
     return 9 * (offset[0] + 1) + 3 * (offset[1] + 1) + offset[2] + 1
 
 
+def fold_of(sizes, slots):
+    merge = sizes[0] == 2
+    lead = 18 * slots
+    shift = -lead % LANES if merge else 0
+    return merge, lead, shift, pl.cdiv(27 * slots + shift, LANES)
+
+
 def kernel(
     sizes,
     stages,
-    pos_ref,
-    spec_ref,
-    nbr_ref,
-    cnt_ref,
-    emb_ref,
-    decay_ref,
-    radial_ref,
-    node_ref,
-    readout_ref,
-    bias_ref,
-    energy_ref,
-    total_ref,
+    pos_any,
+    spec_any,
+    nbr_any,
+    cnt_any,
+    emb_any,
+    decay_any,
+    radial_any,
+    node_any,
+    readout_any,
+    bias_any,
+    out_ref,
     record,
     places,
     hist,
@@ -51,17 +57,31 @@
     feats1,
     *rest,
 ):
+    anys = (
+        pos_any, spec_any, nbr_any, cnt_any, emb_any, decay_any, radial_any, node_any, readout_any, bias_any,
+    )
+    pos_ref, spec_ref, nbr_ref, cnt_ref, emb_ref = rest[:5]
+    decay_ref, radial_ref, node_ref, readout_ref, bias_ref = rest[5:10]
+    load_sem = rest[10]
+    loads = [
+        pltpu.make_async_copy(src, dst, load_sem.at[n])
+        for n, (src, dst) in enumerate(zip(anys, rest[:10]))
+    ]
+    rest = rest[11:]
     stage_bufs = rest[: len(stages)]
     pos_send, pos_recv, hid_send, hid_recv = rest[len(stages) : len(stages) + 4]
     stage_sems = rest[len(stages) + 4 :]
     me = tuple(lax.axis_index(name) for name in AXES)
-    slots = pos_ref.shape[-1]
-    neighbour_count = nbr_ref.shape[-1]
-    features = emb_ref.shape[1]
-    kinds = emb_ref.shape[0]
+    slots = pos_any.shape[-1]
+    neighbour_count = nbr_any.shape[-1]
+    features = emb_any.shape[1]
+    kinds = emb_any.shape[0]
     basis_count = radial_ref.shape[1]
     layers = radial_ref.shape[0]
     tiles = basis.shape[1] // LANES
+    merge, lead, shift_x, tables = fold_of(sizes, slots)
+    first = (lead + shift_x) // LANES
+    kept = lead if merge else 27 * slots
     hi_rows = hist.shape[0] // slots
 
     def device(shift):
@@ -90,8 +110,12 @@
     for shift in sorted(partners):
         pl.semaphore_signal(barrier, inc=1, device_id=device(shift), device_id_type=MESH)
 
+    for n in (0, 1, 3, 2, 4, 5, 6, 7, 8, 9):
+        loads[n].start()
+    for n in (0, 1, 3):
+        loads[n].wait()
     record[...] = jnp.zeros(record.shape, jnp.float32)
-    record[0:3, 0:slots] = pos_ref[0, 0, 0]
+    record[0:3, 0:slots] = pos_ref[0, 0, :, 0]
     record[3:4, 0:slots] = spec_ref[0, 0].astype(jnp.float32)
     record[4:5, 0:slots] = cnt_ref[0, 0].astype(jnp.float32)
     columns = jnp.transpose(record[...])[0:slots]
@@ -118,8 +142,10 @@
     for copy in place_copies:
         copy.start()
 
+    loads[2].wait()
     raw = nbr_ref[0, 0, 0]
     live = lax.broadcasted_iota(jnp.int32, raw.shape, 1).astype(jnp.float32) < count_col
+    raw = jnp.where(raw >= lead, raw + shift_x, raw)
     codes[...] = jnp.where(live, raw, hi_rows * LANES - 1)
     hi_iota = lax.broadcasted_iota(jnp.int32, (hi_rows, neighbour_count), 0)
     lo_iota = lax.broadcasted_iota(jnp.int32, (LANES, neighbour_count), 0)
@@ -131,15 +157,16 @@
             high, low, (((1,), (1,)), ((), ())), preferred_element_type=jnp.float32
         )
 
+    for n in range(4, 10):
+        loads[n].wait()
     own_hidden = jnp.zeros((slots, features), jnp.float32)
     for kind in range(kinds):
         own_hidden = jnp.where(
             species_col == float(kind), emb_ref[kind : kind + 1, :].astype(jnp.float32), own_hidden
         )
     table_rows = feats1.shape[0]
-    feats1[27 * slots : table_rows, :] = jnp.zeros(
-        (table_rows - 27 * slots, features), jnp.bfloat16
-    )
+    if table_rows > kept:
+        feats1[kept:table_rows, :] = jnp.zeros((table_rows - kept, features), jnp.bfloat16)
     emb = emb_ref[...].astype(jnp.float32)
     if kinds < 8:
         emb = jnp.concatenate([emb, jnp.zeros((8 - kinds, features), jnp.float32)], axis=0)
@@ -151,14 +178,15 @@
     for copy in place_copies:
         copy.wait_recv()
 
-    flat = [jnp.zeros((8, LANES), jnp.float32) for _ in range(tiles)]
+    flat = [jnp.zeros((8, LANES), jnp.float32) for _ in range(tables)]
     for off in itertools.product((-1, 0, 1), repeat=3):
         source = tuple(canonical(d, n) for d, n in zip(off, sizes))
         cell = record[...] if source == (0, 0, 0) else places[code_of(source)]
         for component, delta in enumerate(off):
             if delta:
                 cell = jnp.where(sub == component, cell + float(delta), cell)
-        tile, start = divmod(code_of(off) * slots, LANES)
+        column = code_of(off) * slots
+        tile, start = divmod(column + (shift_x if column >= lead else 0), LANES)
         if start:
             cell = pltpu.roll(cell, start, 1)
         stop = start + slots
@@ -168,14 +196,16 @@
 
     for tile in range(tiles):
         span = slice(tile * LANES, (tile + 1) * LANES)
-        r2 = jnp.zeros((slots, LANES), jnp.float32)
-        for c in range(3):
-            delta = flat[tile][c : c + 1, :] - own_pos[c]
-            r2 = r2 + delta * delta
-        times = hist[pl.ds(tile, slots, stride=hi_rows), :]
+        terms = []
+        for part in (tile, tile + first) if merge and tile + first < tables else (tile,):
+            r2 = jnp.zeros((slots, LANES), jnp.float32)
+            for c in range(3):
+                delta = flat[part][c : c + 1, :] - own_pos[c]
+                r2 = r2 + delta * delta
+            terms.append((r2, hist[pl.ds(part, slots, stride=hi_rows), :]))
         for b in range(basis_count):
-            basis[b * slots : (b + 1) * slots, span] = (
-                jnp.exp2(r2 * scales[b]) * times
+            basis[b * slots : (b + 1) * slots, span] = sum(
+                jnp.exp2(r2 * scales[b]) * times for r2, times in terms
             ).astype(jnp.bfloat16)
         one_hot = jnp.where(
             flat[tile][3:4, :].astype(jnp.int32) == sub, 1.0, 0.0
@@ -225,7 +255,7 @@
         copy.wait_recv()
     for off in itertools.product((-1, 0, 1), repeat=3):
         source = tuple(canonical(d, n) for d, n in zip(off, sizes))
-        if source != off:
+        if source != off and code_of(off) * slots < kept:
             feats1[pl.ds(code_of(off) * slots, slots), :] = feats1[
                 pl.ds(code_of(source) * slots, slots), :
             ]
@@ -238,7 +268,7 @@
         readout, padded, (((1,), (1,)), ((), ())), preferred_element_type=jnp.float32
     )
     running = per_atom[0:1, :] + offsets
-    energy_ref[0, 0] = running[:, 0:slots]
+    out_ref[0:1, :] = running
 
     for axes, shifts, buf, send, recv in zip(
         stages, stage_shifts, stage_bufs, stage_sems[0::2], stage_sems[1::2]
@@ -271,7 +301,7 @@
         running = jnp.sum(buf[...], axis=0)
         for copy in copies:
             copy.wait_send()
-    total_ref[...] = jnp.sum(running, axis=1, keepdims=True)
+    out_ref[1:2, :] = jnp.broadcast_to(jnp.sum(running, axis=1, keepdims=True), (1, LANES))
     for copy in place_copies + hidden_copies:
         copy.wait_send()
 
@@ -281,15 +311,15 @@
     slots = positions.shape[-1]
     features = embedding.shape[1]
     basis_count = decay.shape[0]
-    tiles = pl.cdiv(27 * slots, LANES)
-    hi_rows = 16 * pl.cdiv(tiles + 1, 16)
+    merge, lead, _, tables = fold_of(sizes, slots)
+    tiles = pl.cdiv(lead if merge else 27 * slots, LANES)
+    hi_rows = 16 * pl.cdiv(tables + 1, 16)
     devices = math.prod(sizes)
     stages = (AXES,) if devices <= 64 else tuple((name,) for name in AXES)
     stage_ranks = [
         math.prod(n for name, n in zip(AXES, sizes) if name in axes) for axes in stages
     ]
     vmem = pl.BlockSpec(memory_space=pltpu.VMEM)
-    smem = pl.BlockSpec(memory_space=pltpu.SMEM)
     dma = pltpu.SemaphoreType.DMA
     scratch = [
         pltpu.VMEM((8, LANES), jnp.float32),
@@ -304,18 +334,27 @@
     scratch += [dma((27,))] * 4
     for count in stage_ranks:
         scratch += [dma((max(count - 1, 1),))] * 2
-    energy, total = pl.pallas_call(
+    operands = (
+        jnp.transpose(positions, (0, 1, 3, 2, 4)),
+        *args[1:8],
+        readout.reshape(1, features),
+        args[9],
+    )
+    scratch[7:7] = [
+        pltpu.SMEM(x.shape, x.dtype)
+        if x.ndim == 1
+        else pltpu.VMEM(x.shape, x.dtype)
+        for x in operands
+    ] + [dma((len(operands),))]
+    out = pl.pallas_call(
         functools.partial(kernel, sizes, stages),
-        out_shape=(
-            jax.ShapeDtypeStruct(species.shape, jnp.float32),
-            jax.ShapeDtypeStruct((1, 1), jnp.float32),
-        ),
-        in_specs=[vmem, vmem, vmem, vmem, vmem, smem, vmem, vmem, vmem, smem],
-        out_specs=(vmem, vmem),
+        out_shape=jax.ShapeDtypeStruct((2, LANES), jnp.float32),
+        in_specs=[pl.BlockSpec(memory_space=pl.ANY)] * len(operands),
+        out_specs=vmem,
         scratch_shapes=scratch,
         compiler_params=pltpu.CompilerParams(collective_id=0, has_side_effects=True),
-    )(*args[:8], readout.reshape(1, features), args[9])
-    return energy, total.reshape(())
+    )(*operands)
+    return out[0, :slots].reshape(species.shape), out[1, 0]
 
 
 def solution(mesh):

time: 32.1 us -> 28.7 us (0.89)
  between operations: 2.4 us -> 0.64 us
  Pallas kernels: 27.1 us -> 25.5 us
    unnamed x6 -> x2, local copies, waits for them, and re-layouts: 2.39 us -> 0.66 us
    pallas_call x1, Pallas kernels: 27.1 us -> 25.5 us  [body(): pl.pallas_call(functools.partial(kernel, sizes, stages), out_shape=jax.Sh...]
    slice x0 -> x1, local copies, waits for them, and re-layouts: none -> 1.17 us  [body(): return (out[0, :slots].reshape(species.shape), out[1, 0])]
    another operation x0 -> x1, local copies, waits for them, and re-layouts: none -> 0.51 us  [body(): return (out[0, :slots].reshape(species.shape), out[1, 0])]
where the time goes in v2:
time: 28.7 us; the launch traced here: 28.5 us
  Pallas kernels  25.5 us (89%)
  local copies, waits for them, and re-layouts  2.34 us (8%)
  between operations  0.64 us (2%)
    pallas_call x1, Pallas kernels, body(): pl.pallas_call(functools.partial(kernel, sizes, stages), out_shape=jax.Sh...  25.5 us
    slice x1, local copies, waits for them, and re-layouts, body(): return (out[0, :slots].reshape(species.shape), out[1, 0])  1.17 us
    unnamed x2, local copies, waits for them, and re-layouts  0.66 us

profile of v2, /device:TPU:0, one launch (start us, length us, event | category | flops | bytes accessed | tf_op | source)
XLA Modules:
  0.0 28.5 jit_solution(10612930792529177724)
XLA Ops:
  0.6 25.5 %shard_map.113 = f32[2,128]{1,0:T(2,128)} custom-call(f32[1,1,3,1,48]{4,3,2,1,0:T(1,128)} %bitcast.5, s32[1,1,1,48]{3,2,1,0:T(1,128)} %spec_any.1, s32[1,1,1,48,128]{4,3,2,1,0:T(8,128)} %nbr_any.1, s32[1,1,1,48]{3,2,1,0:T(1,128)} %cnt_any.1, bf16[4,128]{1,0:T(4,128)(2,1)} %emb_any.1, f32[16]{0:T(128)} %decay_any.1, bf16[2,16,128]{2,1,0:T(8,128)(2,1)} %radial_any.1, ...), custom_call_target="tpu_custom_call" | custom-call | tf_op jit(solution)/shard_map/pallas_call | solution.py:349
  26.2 1.2 %slice.7 = f32[1,1]{1,0:T(1,128)} slice(f32[2,128]{1,0:T(2,128)} %shard_map.113), slice={[1:2], [0:1]} | slice | bytes 8 | tf_op jit(solution)/shard_map/slice | solution.py:357
  27.3 0.0 copy-start
  27.3 0.7 %copy-done = f32[2,128]{1,0:T(2,128)S(1)} copy-done((f32[2,128]{1,0:T(2,128)S(1)}, f32[2,128]{1,0:T(2,128)}, u32[]{:S(2)}) %copy-start) | copy-done | bytes 1048
  28.0 0.5 %slice_bitcast_fusion = f32[1,1,1,48]{3,2,1,0:T(1,128)} fusion(f32[2,128]{1,0:T(2,128)S(1)} %copy-done), kind=kLoop, calls=%fused_computation | loop fusion | bytes 384 | tf_op jit(solution)/shard_map/reshape;squeeze | solution.py:357
Async XLA Ops:
  27.3 0.7 %copy-start = (f32[2,128]{1,0:T(2,128)S(1)}, f32[2,128]{1,0:T(2,128)}, u32[]{:S(2)}) copy-start(f32[2,128]{1,0:T(2,128)} %shard_map.113) | copy-start | bytes 3076

commit v3 on v2

--- a/solution.py
+++ b/solution.py
@@ -117,8 +117,12 @@
     record[...] = jnp.zeros(record.shape, jnp.float32)
     record[0:3, 0:slots] = pos_ref[0, 0, :, 0]
     record[3:4, 0:slots] = spec_ref[0, 0].astype(jnp.float32)
-    record[4:5, 0:slots] = cnt_ref[0, 0].astype(jnp.float32)
-    columns = jnp.transpose(record[...])[0:slots]
+    counts = jnp.concatenate(
+        [cnt_ref[0, 0].astype(jnp.float32), jnp.zeros((1, LANES - slots), jnp.float32)], axis=1
+    )
+    columns = jnp.transpose(
+        jnp.concatenate([record[...], counts, jnp.zeros((3, LANES), jnp.float32)], axis=0)
+    )[0:slots]
     own_pos = [
         jnp.broadcast_to(columns[:, c : c + 1], (slots, LANES)) for c in range(3)
     ]
@@ -178,21 +182,23 @@
     for copy in place_copies:
         copy.wait_recv()
 
-    flat = [jnp.zeros((8, LANES), jnp.float32) for _ in range(tables)]
+    flat = [jnp.zeros((4, LANES), jnp.float32) for _ in range(tables)]
+    lane4 = lane[0:4]
+    sub4 = sub[0:4]
     for off in itertools.product((-1, 0, 1), repeat=3):
         source = tuple(canonical(d, n) for d, n in zip(off, sizes))
         cell = record[...] if source == (0, 0, 0) else places[code_of(source)]
         for component, delta in enumerate(off):
             if delta:
-                cell = jnp.where(sub == component, cell + float(delta), cell)
+                cell = jnp.where(sub4 == component, cell + float(delta), cell)
         column = code_of(off) * slots
         tile, start = divmod(column + (shift_x if column >= lead else 0), LANES)
         if start:
             cell = pltpu.roll(cell, start, 1)
         stop = start + slots
-        flat[tile] = jnp.where((lane >= start) & (lane < stop), cell, flat[tile])
+        flat[tile] = jnp.where((lane4 >= start) & (lane4 < stop), cell, flat[tile])
         if stop > LANES:
-            flat[tile + 1] = jnp.where(lane < stop - LANES, cell, flat[tile + 1])
+            flat[tile + 1] = jnp.where(lane4 < stop - LANES, cell, flat[tile + 1])
 
     for tile in range(tiles):
         span = slice(tile * LANES, (tile + 1) * LANES)
@@ -322,8 +328,8 @@
     vmem = pl.BlockSpec(memory_space=pltpu.VMEM)
     dma = pltpu.SemaphoreType.DMA
     scratch = [
-        pltpu.VMEM((8, LANES), jnp.float32),
-        pltpu.VMEM((27, 8, LANES), jnp.float32),
+        pltpu.VMEM((4, LANES), jnp.float32),
+        pltpu.VMEM((27, 4, LANES), jnp.float32),
         pltpu.VMEM((slots * hi_rows, LANES), jnp.float32),
         pltpu.VMEM((slots, neighbours.shape[-1]), jnp.int32),
         pltpu.VMEM((basis_count * slots, tiles * LANES), jnp.bfloat16),
@@ -348,7 +354,7 @@
     ] + [dma((len(operands),))]
     out = pl.pallas_call(
         functools.partial(kernel, sizes, stages),
-        out_shape=jax.ShapeDtypeStruct((2, LANES), jnp.float32),
+        out_shape=pltpu.VMEM((2, LANES), jnp.float32),
         in_specs=[pl.BlockSpec(memory_space=pl.ANY)] * len(operands),
         out_specs=vmem,
         scratch_shapes=scratch,

time: 28.7 us -> 26.5 us (0.923)
  local copies, waits for them, and re-layouts: 2.34 us -> 1.02 us
  Pallas kernels: 25.5 us -> 24.7 us
    pallas_call x1, Pallas kernels: 25.5 us -> 24.7 us  [body(): pl.pallas_call(functools.partial(kernel, sizes, stages), out_shape=pltpu....]
    unnamed x2 -> x0, local copies, waits for them, and re-layouts: 0.66 us -> none
    slice x1, local copies, waits for them, and re-layouts: 1.17 us -> 0.51 us  [body(): return (out[0, :slots].reshape(species.shape), out[1, 0])]
where the time goes in v3:
time: 26.5 us; the launch traced here: 26.4 us
  Pallas kernels  24.7 us (93%)
  local copies, waits for them, and re-layouts  1.02 us (4%)
  between operations  0.64 us (2%)
    pallas_call x1, Pallas kernels, body(): pl.pallas_call(functools.partial(kernel, sizes, stages), out_shape=pltpu....  24.7 us

profile of v3, /device:TPU:0, one launch (start us, length us, event | category | flops | bytes accessed | tf_op | source)
XLA Modules:
  0.0 26.4 jit_solution(3180903612957523434)
XLA Ops:
  0.6 24.7 %shard_map.113 = f32[2,128]{1,0:T(2,128)S(1)} custom-call(f32[1,1,3,1,48]{4,3,2,1,0:T(1,128)} %bitcast.5, s32[1,1,1,48]{3,2,1,0:T(1,128)} %spec_any.1, s32[1,1,1,48,128]{4,3,2,1,0:T(8,128)} %nbr_any.1, s32[1,1,1,48]{3,2,1,0:T(1,128)} %cnt_any.1, bf16[4,128]{1,0:T(4,128)(2,1)} %emb_any.1, f32[16]{0:T(128)} %decay_any.1, bf16[2,16,128]{2,1,0:T(8,128)(2,1)} %radial_any.1, ...), custom_call_target="tpu_custom_call" | custom-call | tf_op jit(solution)/shard_map/pallas_call | solution.py:355
  25.3 0.5 %slice.7 = f32[1,1]{1,0:T(1,128)} slice(f32[2,128]{1,0:T(2,128)S(1)} %shard_map.113), slice={[1:2], [0:1]} | slice | bytes 8 | tf_op jit(solution)/shard_map/slice | solution.py:363
  25.9 0.5 %slice_bitcast_fusion = f32[1,1,1,48]{3,2,1,0:T(1,128)} fusion(f32[2,128]{1,0:T(2,128)S(1)} %shard_map.113), kind=kLoop, calls=%fused_computation | loop fusion | bytes 384 | tf_op jit(solution)/shard_map/reshape;squeeze | solution.py:363

commit v4 on v3

--- a/solution.py
+++ b/solution.py
@@ -28,7 +28,7 @@
 
 
 def fold_of(sizes, slots):
-    merge = sizes[0] == 2
+    merge = False
     lead = 18 * slots
     shift = -lead % LANES if merge else 0
     return merge, lead, shift, pl.cdiv(27 * slots + shift, LANES)
@@ -221,11 +221,19 @@
         ).astype(jnp.bfloat16)
 
     def interaction(layer, feats, hidden):
-        collected = jnp.dot(basis[...], feats[...], preferred_element_type=jnp.float32)
         weight = radial_ref[layer].astype(jnp.float32)
         message = jnp.zeros((slots, features), jnp.float32)
-        for b in range(basis_count):
-            message = message + collected[b * slots : (b + 1) * slots] * weight[b : b + 1]
+        step = basis_count // 4
+        for lead_b in range(0, basis_count, step):
+            collected = jnp.dot(
+                basis[lead_b * slots : (lead_b + step) * slots, :],
+                feats[...],
+                preferred_element_type=jnp.float32,
+            )
+            for b in range(step):
+                message = message + (
+                    collected[b * slots : (b + 1) * slots] * weight[lead_b + b : lead_b + b + 1]
+                )
         inv_scale = lax.rsqrt(jnp.mean(message * message, axis=-1, keepdims=True) + 1e-05)
         normed = (message * inv_scale).astype(jnp.bfloat16)
         value = jnp.dot(normed, node_ref[layer], preferred_element_type=jnp.float32)

time: 26.5 us -> 26.6 us (level)
  no operation moved by 1% of the time
where the time goes in v4:
time: 26.6 us; the launch traced here: 26.4 us
  Pallas kernels  24.8 us (93%)
  local copies, waits for them, and re-layouts  1.02 us (4%)
  between operations  0.64 us (2%)
    pallas_call x1, Pallas kernels, body(): pl.pallas_call(functools.partial(kernel, sizes, stages), out_shape=pltpu....  24.8 us

profile of v4, /device:TPU:0, one launch (start us, length us, event | category | flops | bytes accessed | tf_op | source)
XLA Modules:
  0.0 26.4 jit_solution(15676987550159107436)
XLA Ops:
  0.6 24.8 %shard_map.113 = f32[2,128]{1,0:T(2,128)S(1)} custom-call(f32[1,1,3,1,48]{4,3,2,1,0:T(1,128)} %bitcast.5, s32[1,1,1,48]{3,2,1,0:T(1,128)} %spec_any.1, s32[1,1,1,48,128]{4,3,2,1,0:T(8,128)} %nbr_any.1, s32[1,1,1,48]{3,2,1,0:T(1,128)} %cnt_any.1, bf16[4,128]{1,0:T(4,128)(2,1)} %emb_any.1, f32[16]{0:T(128)} %decay_any.1, bf16[2,16,128]{2,1,0:T(8,128)(2,1)} %radial_any.1, ...), custom_call_target="tpu_custom_call" | custom-call | tf_op jit(solution)/shard_map/pallas_call | solution.py:363
  25.4 0.5 %slice.7 = f32[1,1]{1,0:T(1,128)} slice(f32[2,128]{1,0:T(2,128)S(1)} %shard_map.113), slice={[1:2], [0:1]} | slice | bytes 8 | tf_op jit(solution)/shard_map/slice | solution.py:371
  25.9 0.5 %slice_bitcast_fusion = f32[1,1,1,48]{3,2,1,0:T(1,128)} fusion(f32[2,128]{1,0:T(2,128)S(1)} %shard_map.113), kind=kLoop, calls=%fused_computation | loop fusion | bytes 384 | tf_op jit(solution)/shard_map/reshape;squeeze | solution.py:371
